TPU v7x, 256 devices: a whole 4x4x8 slice. The times are simulated.
256 devices in a mesh: slab: 128 (over z, y, x), feat: 2 (over core).
Axes of the slice: x: 4, y: 4, z: 8, core: 2. Of those that a mesh axis runs over, the one named last changes fastest.
Arguments:
- states: float32 [40, 65536], P(None, ('slab', 'feat')), may hold values from -6 to 6
- inputs: float32 [65536], P(('slab', 'feat')), may hold values from -4 to 4
- targets: float32 [40, 65536], P(None, ('slab', 'feat')), may hold values from -4 to 4
Outputs:
- local_operators: float32 [128, 40, 862], P('slab', 'feat')
- scaled_duals: float32 [128, 40, 862], P('slab', 'feat')
- consensus: float32 [40, 862], P('feat')
- residual_history: float32 [2, 2], replicated
All inputs are finite; a program needn't handle non-finite values.
Results may differ from a plain program's by a relative error of at most 0.0003.
Values sent between devices are 32-bit elements; how exact they have to be, the bound alone decides.
A program may use at most 64 MiB of HBM per device.

v0:
```python
import jax
import jax.numpy as jnp
from jax import lax
from jax.sharding import Mesh
from jax.sharding import PartitionSpec as P

ITERS = 2
SLAB = ("slab_0", "slab_1", "slab_2")
SLAB_FEAT = ("slab_0", "slab_1", "slab_2", "feat")
penalty = 1.0


def total_of_pieces(array, axis):
    tiles = lax.all_gather(array, axis)
    return tiles.sum(axis=0)


def rows_first(arrays, axis, dims):
    turned = [jnp.moveaxis(a, dim, 0) for a, dim in zip(arrays, dims)]
    widths = [t[0].size for t in turned]
    both = jnp.concatenate([t.reshape(-1, w) for t, w in zip(turned, widths)], axis=1)
    whole = lax.all_gather(both, axis, axis=0, tiled=True)
    tiles = jnp.split(whole, [sum(widths[:k]) for k in range(1, len(widths))], axis=1)
    return tuple(
        (
            jnp.moveaxis(b.reshape(-1, *t.shape[1:]), 0, dim)
            for b, t, dim in zip(tiles, turned, dims)
        )
    )


def by_axis(array, axes):
    for axis in axes:
        array = lax.psum(array, axis)
    return array


def features(states, inputs):
    reduced = states.shape[0]
    blocks = [states]
    for column in range(reduced):
        blocks.append(states[column : column + 1] * states[column:])
    blocks.append(inputs[None, :])
    blocks.append(jnp.ones_like(inputs)[None, :])
    return jnp.concatenate(blocks, 0)


def product(left, right):
    return jnp.dot(left, right, precision=lax.Precision.HIGHEST, preferred_element_type=jnp.float32)


def solve_rows(factor, right_side):
    return jax.scipy.linalg.cho_solve((factor, True), right_side.T).T


def slab_average(summand):
    return total_of_pieces(summand, SLAB)


def shards(states, inputs, targets):
    reduced = states.shape[0]
    feat_count = lax.axis_size("feat")
    slab_count = lax.axis_size(SLAB)
    half_rows = reduced // feat_count
    all_states, all_targets, all_inputs = rows_first((states, targets, inputs), "feat", (1, 1, 0))
    design = features(all_states, all_inputs)
    row_total = design.shape[1]
    gram_matrix = product(design, design.T) / row_total
    first_row = lax.axis_index("feat") * half_rows
    picked = lax.dynamic_slice_in_dim(all_targets, first_row, half_rows, 0)
    cross = product(picked, design.T) / row_total
    width = gram_matrix.shape[0]
    factor = jnp.linalg.cholesky(gram_matrix + penalty * jnp.eye(width, dtype=jnp.float32))
    consensus = jnp.zeros((half_rows, width), jnp.float32)
    duals = jnp.zeros((half_rows, width), jnp.float32)
    operator_rows = duals
    primal_list = []
    dual_list = []
    for sweep in range(ITERS):
        operator_rows = solve_rows(factor, cross + penalty * (consensus - duals))
        updated = slab_average(operator_rows + duals) / slab_count
        duals = duals + operator_rows - updated
        primal_part = jnp.sum(jnp.square(operator_rows - updated))
        dual_part = penalty * penalty * jnp.sum(jnp.square(updated - consensus))
        primal_sum, dual_sum = (by_axis(primal_part, SLAB_FEAT), by_axis(dual_part, SLAB_FEAT))
        primal_list.append(primal_sum)
        dual_list.append(dual_sum)
        consensus = updated
    history = jnp.stack([jnp.stack(primal_list), jnp.stack(dual_list)])
    residual_history = jnp.sqrt(history / (slab_count * reduced * width))
    return (operator_rows[None], duals[None], consensus, residual_history)


def solution(mesh):
    split = Mesh(
        mesh.devices.reshape(8, 4, 4, mesh.shape["feat"]), ("slab_0", "slab_1", "slab_2", "feat")
    )
    return jax.shard_map(
        shards,
        mesh=split,
        in_specs=(P(None, SLAB_FEAT), P(SLAB_FEAT), P(None, SLAB_FEAT)),
        out_specs=(P(SLAB, "feat", None), P(SLAB, "feat", None), P("feat", None), P()),
        check_vma=False,
    )
```

profile of v0, /device:TPU:1, one launch (start us, length us, event | category | flops | bytes accessed | tf_op | source)
XLA Modules:
  0.0 660.4 jit_solution(3695795320718135102)
XLA Ops:
  8.6 4.8 all_gather.15
  24.2 13.3 %concatenate.49 = f32[862,512]{1,0:T(8,128)S(1)} concatenate(f32[40,512]{1,0:T(8,128)S(1)} %get-tuple-element.61, f32[40,512]{1,0:T(8,128)S(1)} %broadcast_multiply_fusion.1, f32[39,512]{1,0:T(8,128)S(1)} %slice_multiply_fusion.6, f32[38,512]{1,0:T(8,128)S(1)} %slice_multiply_fusion.5, f32[37,512]{1,0:T(8,128)S(1)} %slice_multiply_fusion.4, f32[36,512]{1,0:T(8,128)S(1)} %slice_multiply_fusion.3, ...), dimensions={0} | concatenate | bytes 3530752 | tf_op jit(solution)/shard_map/concatenate | solution.py:45
  37.5 7.8 %convert_add_fusion = (f32[862,862]{0,1:T(8,128)}, f32[862,862]{0,1:T(8,128)}) fusion(f32[862,512]{1,0:T(8,128)S(1)} %concatenate.49), kind=kOutput, calls=%fused_computation.8 | convolution fusion | flops 4568234496 | bytes 7709728 | tf_op jit(solution)/shard_map/dot_general | solution.py:49
  45.4 3.6 copy.12
  49.0 2.3 fusion.1
  51.3 1.6 copy-done.3
  52.9 11.7 %cholesky.196 = f32[128,128]{1,0:T(8,128)S(1)} custom-call(f32[128,128]{1,0:T(8,128)S(1)} %cholesky.508), custom_call_target="Cholesky" | custom-call | tf_op jit(solution)/shard_map/jit(cholesky)/cholesky | solution.py:73
  64.7 9.8 %custom-call.56 = f32[1,128,128]{1,2,0:T(8,128)S(1)} custom-call(f32[1,128,128]{2,1,0:T(8,128)S(1)} %get-tuple-element.118), custom_call_target="InvertDiagBlocksLowerTriangular" | custom-call | tf_op jit(solution)/shard_map/jit(cholesky)/cholesky | solution.py:73
  74.7 1.4 constant_dynamic-update-slice_fusion.62
  76.1 1.5 convolution_subtract_fusion
  78.2 13.2 %cholesky.217 = f32[128,128]{1,0:T(8,128)} custom-call(f32[128,128]{1,0:T(8,128)} %cholesky.512), custom_call_target="Cholesky" | custom-call | tf_op jit(solution)/shard_map/jit(cholesky)/cholesky | solution.py:73
  91.4 1.5 select_reduce_fusion.4
  92.9 11.7 %custom-call.57 = f32[1,128,128]{1,2,0:T(8,128)} custom-call(f32[1,128,128]{2,1,0:T(8,128)} %get-tuple-element.115), custom_call_target="InvertDiagBlocksLowerTriangular" | custom-call | tf_op jit(solution)/shard_map/jit(cholesky)/cholesky | solution.py:73
  104.6 1.2 convolution_dynamic-update-slice_fusion
  105.8 1.6 convolution_subtract_fusion.1
  107.4 12.3 %cholesky.413 = f32[128,128]{1,0:T(8,128)} custom-call(f32[128,128]{1,0:T(8,128)S(1)} %cholesky.517), custom_call_target="Cholesky" | custom-call | tf_op jit(solution)/shard_map/jit(cholesky)/cholesky | solution.py:73
  121.4 10.4 %custom-call.58 = f32[1,128,128]{1,2,0:T(8,128)} custom-call(f32[1,128,128]{2,1,0:T(8,128)S(1)} %get-tuple-element.112), custom_call_target="InvertDiagBlocksLowerTriangular" | custom-call | tf_op jit(solution)/shard_map/jit(cholesky)/cholesky | solution.py:73
  133.0 1.7 convolution_subtract_fusion.2
  134.7 11.9 %cholesky.432 = f32[128,128]{1,0:T(8,128)S(1)} custom-call(f32[128,128]{1,0:T(8,128)S(1)} %cholesky.522), custom_call_target="Cholesky" | custom-call | tf_op jit(solution)/shard_map/jit(cholesky)/cholesky | solution.py:73
  147.3 9.8 %custom-call.59 = f32[1,128,128]{1,2,0:T(8,128)S(1)} custom-call(f32[1,128,128]{2,1,0:T(8,128)S(1)} %get-tuple-element.109), custom_call_target="InvertDiagBlocksLowerTriangular" | custom-call | tf_op jit(solution)/shard_map/jit(cholesky)/cholesky | solution.py:73
  157.4 1.7 convolution_subtract_fusion.3
  159.1 11.7 %cholesky.451 = f32[128,128]{1,0:T(8,128)S(1)} custom-call(f32[128,128]{1,0:T(8,128)S(1)} %cholesky.527), custom_call_target="Cholesky" | custom-call | tf_op jit(solution)/shard_map/jit(cholesky)/cholesky | solution.py:73
  171.6 9.8 %custom-call.60 = f32[1,128,128]{1,2,0:T(8,128)S(1)} custom-call(f32[1,128,128]{2,1,0:T(8,128)S(1)} %get-tuple-element.106), custom_call_target="InvertDiagBlocksLowerTriangular" | custom-call | tf_op jit(solution)/shard_map/jit(cholesky)/cholesky | solution.py:73
  181.7 1.5 convolution_subtract_fusion.4
  183.2 11.9 %cholesky.471 = f32[128,128]{1,0:T(8,128)S(1)} custom-call(f32[128,128]{1,0:T(8,128)S(1)} %cholesky.532), custom_call_target="Cholesky" | custom-call | tf_op jit(solution)/shard_map/jit(cholesky)/cholesky | solution.py:73
  195.8 9.8 %custom-call.61 = f32[1,128,128]{1,2,0:T(8,128)S(1)} custom-call(f32[1,128,128]{2,1,0:T(8,128)S(1)} %get-tuple-element.103), custom_call_target="InvertDiagBlocksLowerTriangular" | custom-call | tf_op jit(solution)/shard_map/jit(cholesky)/cholesky | solution.py:73
  207.0 8.6 %cholesky.492 = f32[94,94]{1,0:T(8,128)S(1)} custom-call(f32[94,94]{1,0:T(8,128)S(1)} %convolution_subtract_fusion.5), custom_call_target="Cholesky" | custom-call | tf_op jit(solution)/shard_map/jit(cholesky)/cholesky | solution.py:73
  223.3 18.0 %while.4 = (s32[]{:T(128)}, f32[862,862]{1,0:T(8,128)}, s32[6,2]{0,1:T(2,128)S(1)}, f32[6,128,128]{2,1,0:T(8,128)S(1)}, s32[]{:T(128)}) while((s32[]{:T(128)}, f32[862,862]{1,0:T(8,128)}, s32[6,2]{0,1:T(2,128)S(1)}, f32[6,128,128]{2,1,0:T(8,128)S(1)}, s32[]{:T(128)}) %tuple.121), condition=%wide.while_cond.clone, body=%wide.while_body.clone.sunk | while | flops 2 | bytes 131189 | solution.py:53
  224.0 2.3 bitcast_dynamic-update-slice_fusion.2
  227.0 2.3 bitcast_dynamic-update-slice_fusion.2
  230.0 2.3 bitcast_dynamic-update-slice_fusion.2
  233.0 2.3 bitcast_dynamic-update-slice_fusion.2
  236.0 2.3 bitcast_dynamic-update-slice_fusion.2
  239.0 2.3 bitcast_dynamic-update-slice_fusion.2
  243.2 69.8 %custom-call.64 = f32[7,128,128]{1,2,0:T(8,128)S(1)} custom-call(f32[7,128,128]{2,1,0:T(8,128)} %pad_maximum_fusion), custom_call_target="InvertDiagBlocksLowerTriangular" | custom-call | tf_op jit(solution)/shard_map/jit(_cho_solve)/triangular_solve | solution.py:53
  313.1 3.1 convolution_multiply_fusion
  327.0 131.4 %all-gather.7.cloned.1.call-done = f32[128,20,862]{2,1,0:T(8,128)} async-done(((f32[1,20,862]{2,1,0:T(8,128)}), f32[128,20,862]{2,1,0:T(8,128)}) %all-gather.7.cloned.1.call-update) | async-done | bytes 8826896 | tf_op jit(solution)/shard_map/all_gather | solution.py:14
  458.4 5.4 reduce_sum.54
  471.4 1.5 fusion.108
  473.7 127.5 %all-gather.9.cloned.1.call-done = f32[128,20,862]{2,1,0:T(8,128)} async-done(((f32[1,20,862]{2,1,0:T(8,128)}), f32[128,20,862]{2,1,0:T(8,128)}) %all-gather.9.cloned.1.call-update) | async-done | bytes 8826896 | tf_op jit(solution)/shard_map/all_gather | solution.py:14
  601.2 4.8 reduce_sum.55
  606.0 1.6 multiply_reduce_fusion.2
  609.2 12.5 %all-reduce.3 = (f32[]{:T(128)}, f32[]{:T(128)}, f32[]{:T(128)}, f32[]{:T(128)}) all-reduce(f32[]{:T(128)} %get-tuple-element.31, f32[]{:T(128)} %get-tuple-element.30, f32[]{:T(128)} %get-tuple-element.32, f32[]{:T(128)} %get-tuple-element.29), channel_id=1, replica_groups=mesh['slab_0'=8,'slab_1'=4,'slab_2'=4,'feat'=2] {'slab_0'}, use_global_device_ids=true, to_apply=%region_32.34 | all-reduce | flops 4 | bytes 32 | tf_op jit(solution)/shard_map/psum | solution.py:34
  621.7 9.1 %all-reduce.5 = (f32[]{:T(128)}, f32[]{:T(128)}, f32[]{:T(128)}, f32[]{:T(128)}) all-reduce(f32[]{:T(128)} %get-tuple-element.41, f32[]{:T(128)} %get-tuple-element.42, f32[]{:T(128)} %get-tuple-element.43, f32[]{:T(128)} %get-tuple-element.44), channel_id=1, replica_groups=mesh['slab_0'=8,'slab_1'=4,'slab_2'=4,'feat'=2] {'slab_1'}, use_global_device_ids=true, to_apply=%region_33.35 | all-reduce | flops 4 | bytes 32 | tf_op jit(solution)/shard_map/psum | solution.py:34
  630.8 7.2 %all-reduce.4 = (f32[]{:T(128)}, f32[]{:T(128)}, f32[]{:T(128)}, f32[]{:T(128)}) all-reduce(f32[]{:T(128)} %get-tuple-element.49, f32[]{:T(128)} %get-tuple-element.50, f32[]{:T(128)} %get-tuple-element.51, f32[]{:T(128)} %get-tuple-element.52), channel_id=1, replica_groups=mesh['slab_0'=8,'slab_1'=4,'slab_2'=4,'feat'=2] {'slab_2'}, use_global_device_ids=true, to_apply=%region_34.36 | all-reduce | flops 4 | bytes 32 | tf_op jit(solution)/shard_map/psum | solution.py:34
  638.0 11.9 %all-reduce.6 = (f32[1]{0:T(128)}, f32[1]{0:T(128)}, f32[1]{0:T(128)}, f32[1]{0:T(128)}) all-reduce(f32[1]{0:T(128)} %bitcast.84, f32[1]{0:T(128)} %bitcast.83, f32[1]{0:T(128)} %bitcast.81, f32[1]{0:T(128)} %bitcast.80), channel_id=1, replica_groups=mesh['slab_0'=8,'slab_1'=4,'slab_2'=4,'feat'=2] {'feat'}, use_global_device_ids=true, to_apply=%region_35.37 | all-reduce | flops 4 | bytes 32 | tf_op jit(solution)/shard_map/psum | solution.py:34
  649.9 1.3 maximum_bitcast_fusion.1
  651.2 1.3 maximum_bitcast_fusion
  (201 shorter events, 49.8 us)
Async XLA Ops:
  7.2 451.2 %all-gather.7.cloned.1.call-start = ((), (), s32[]{:S(2)}) async-start(), calls=%async_computation | async-start | bytes 11096064 | tf_op jit(solution)/shard_map/all_gather | solution.py:14
  37.5 7.8 %copy-start = (f32[862,512]{1,0:T(8,128)}, f32[862,512]{1,0:T(8,128)S(1)}, u32[]{:S(2)}) copy-start(f32[862,512]{1,0:T(8,128)S(1)} %concatenate.49) | copy-start | bytes 5296132
  51.3 1.6 copy-start.3
  221.4 0.9 copy-start.9
  221.4 1.9 copy-start.7
  221.7 1.7 copy-start.1
  241.4 75.0 %copy-start.2 = (f32[862,862]{1,0:T(8,128)S(1)}, f32[862,862]{1,0:T(8,128)}, u32[]{:S(2)}) copy-start(f32[862,862]{1,0:T(8,128)} %get-tuple-element.215) | copy-start | bytes 8916532
  316.1 10.8 %copy-start.6 = (f32[862,20]{0,1:T(8,128)}, f32[862,20]{0,1:T(8,128)S(1)}, u32[]{:S(2)}) copy-start(f32[862,20]{0,1:T(8,128)S(1)} %convolution_multiply_fusion) | copy-start | bytes 206884
  327.0 274.3 %all-gather.9.cloned.1.call-start = ((), (), s32[]{:S(2)}) async-start(), calls=%async_computation.1 | async-start | bytes 11096064 | tf_op jit(solution)/shard_map/all_gather | solution.py:14
  463.7 7.6 %copy-start.4 = (f32[20,862]{1,0:T(8,128)S(1)}, f32[20,862]{1,0:T(8,128)}, u32[]{:S(2)}) copy-start(f32[20,862]{1,0:T(8,128)} %reduce_sum.54) | copy-start | bytes 206884
  473.7 132.3 %copy-start.5 = (f32[20,862]{1,0:T(8,128)S(1)}, f32[20,862]{1,0:T(8,128)}, u32[]{:S(2)}) copy-start(f32[20,862]{1,0:T(8,128)} %reduce_sum.54) | copy-start | bytes 206884
  607.6 45.6 %copy-start.8 = (f32[20,862]{1,0:T(8,128)}, f32[20,862]{1,0:T(8,128)S(1)}, u32[]{:S(2)}) copy-start(f32[20,862]{1,0:T(8,128)S(1)} %get-tuple-element.57) | copy-start | bytes 206884
Sparse Core Ops, SparseCore 0:
  327.1 131.2 all-gather.6
  473.1 128.0 all-gather.8
where the time goes:
time: 667 us; the launch traced here: 660 us
  waiting for transfers between devices  259 us (39%)
  other arithmetic  252 us (38%)
  local copies, waits for them, and re-layouts  46.1 us (7%)
  blocking collectives  45.4 us (7%)
  matrix products  37.7 us (6%)
  between operations  20 us (3%)
    all_gather x2, waiting for transfers between devices, total_of_pieces(): tiles = lax.all_gather(array, axis)  259 us
    another operation x26, other arithmetic, shards(): jnp.linalg.cholesky(gram_matrix + penalty * jnp.eye(width, dtype=jnp.floa...  149 us
    another operation x8, other arithmetic, solve_rows(): return jax.scipy.linalg.cho_solve((factor, True), right_side.T).T  72.5 us
    psum x4, blocking collectives, by_axis(): array = lax.psum(array, axis)  40.7 us
    another operation x26, local copies, waits for them, and re-layouts, solve_rows(): return jax.scipy.linalg.cho_solve((factor, True), right_side.T).T  19.2 us
    another operation x12, matrix products, shards(): jnp.linalg.cholesky(gram_matrix + penalty * jnp.eye(width, dtype=jnp.floa...  13.7 us
  transfers between devices with their start and end apart: 2, of which 2 were waited for; matrix products, arithmetic and copies ran while one was open for 0% of the time, Pallas kernels for 0%

commit v1 on v0

--- a/solution.py
+++ b/solution.py
@@ -31,7 +31,7 @@
 
 def by_axis(array, axes):
     for axis in axes:
-        array = lax.psum(array, axis)
+        array = jnp.sum(lax.all_gather(array, axis), axis=0)
     return array
 
 

time: 667 us -> 689 us (1.033)
  local copies, waits for them, and re-layouts: 46.1 us -> 70.8 us
    psum x4 -> x0, blocking collectives: 40.7 us -> none  [by_axis(): array = lax.psum(array, axis)]
    unnamed x0 -> x4, blocking collectives: none -> 37.9 us
    unnamed x46 -> x86, local copies, waits for them, and re-layouts: 7.24 us -> 34.4 us
    reduce_sum x0 -> x16, other arithmetic: none -> 9.77 us  [by_axis(): array = jnp.sum(lax.all_gather(array, axis), axis=0)]
  transfers between devices with their start and end apart: 2 -> 2, of which waited for: 2 -> 2; matrix products, arithmetic and copies ran while one was open for 0% -> 1% of each run, Pallas kernels for 0% -> 0%
where the time goes in v1:
time: 689 us; the launch traced here: 682 us
  other arithmetic  256 us (37%)
  waiting for transfers between devices  256 us (37%)
  local copies, waits for them, and re-layouts  70.8 us (10%)
  blocking collectives  42.6 us (6%)
  matrix products  36.1 us (5%)
  between operations  19.9 us (3%)
    all_gather x2, waiting for transfers between devices, total_of_pieces(): tiles = lax.all_gather(array, axis)  256 us
    another operation x26, other arithmetic, shards(): jnp.linalg.cholesky(gram_matrix + penalty * jnp.eye(width, dtype=jnp.floa...  145 us
    another operation x8, other arithmetic, solve_rows(): return jax.scipy.linalg.cho_solve((factor, True), right_side.T).T  72.2 us
    unnamed x4, blocking collectives  37.9 us
    unnamed x86, local copies, waits for them, and re-layouts  34.4 us
    another operation x26, local copies, waits for them, and re-layouts, solve_rows(): return jax.scipy.linalg.cho_solve((factor, True), right_side.T).T  18 us
  transfers between devices with their start and end apart: 2, of which 2 were waited for; matrix products, arithmetic and copies ran while one was open for 1% of the time, Pallas kernels for 0%

profile of v1, /device:TPU:1, one launch (start us, length us, event | category | flops | bytes accessed | tf_op | source)
XLA Modules:
  0.0 681.7 jit_solution(10247175323940923915)
XLA Ops:
  8.0 4.8 all_gather.111
  23.6 11.9 %concatenate.49 = f32[862,512]{1,0:T(8,128)S(1)} concatenate(f32[40,512]{1,0:T(8,128)S(1)} %get-tuple-element.61, f32[40,512]{1,0:T(8,128)S(1)} %broadcast_multiply_fusion.1, f32[39,512]{1,0:T(8,128)S(1)} %slice_multiply_fusion.6, f32[38,512]{1,0:T(8,128)S(1)} %slice_multiply_fusion.5, f32[37,512]{1,0:T(8,128)S(1)} %slice_multiply_fusion.4, f32[36,512]{1,0:T(8,128)S(1)} %slice_multiply_fusion.3, ...), dimensions={0} | concatenate | bytes 3530752 | tf_op jit(solution)/shard_map/concatenate | solution.py:45
  35.5 7.8 %convert_add_fusion = (f32[862,862]{0,1:T(8,128)}, f32[862,862]{0,1:T(8,128)}) fusion(f32[862,512]{1,0:T(8,128)S(1)} %concatenate.49), kind=kOutput, calls=%fused_computation.8 | convolution fusion | flops 4568234496 | bytes 7709728 | tf_op jit(solution)/shard_map/dot_general | solution.py:49
  43.3 3.9 copy.12
  47.2 2.3 fusion.1
  49.4 1.6 copy-done.3
  51.1 11.7 %cholesky.196 = f32[128,128]{1,0:T(8,128)S(1)} custom-call(f32[128,128]{1,0:T(8,128)S(1)} %cholesky.508), custom_call_target="Cholesky" | custom-call | tf_op jit(solution)/shard_map/jit(cholesky)/cholesky | solution.py:73
  63.0 9.8 %custom-call.56 = f32[1,128,128]{1,2,0:T(8,128)S(1)} custom-call(f32[1,128,128]{2,1,0:T(8,128)S(1)} %get-tuple-element.118), custom_call_target="InvertDiagBlocksLowerTriangular" | custom-call | tf_op jit(solution)/shard_map/jit(cholesky)/cholesky | solution.py:73
  72.9 1.4 constant_dynamic-update-slice_fusion.62
  74.3 1.5 convolution_subtract_fusion
  76.4 12.5 %cholesky.217 = f32[128,128]{1,0:T(8,128)S(1)} custom-call(f32[128,128]{1,0:T(8,128)} %cholesky.512), custom_call_target="Cholesky" | custom-call | tf_op jit(solution)/shard_map/jit(cholesky)/cholesky | solution.py:73
  89.6 10.8 %custom-call.57 = f32[1,128,128]{1,2,0:T(8,128)S(1)} custom-call(f32[1,128,128]{2,1,0:T(8,128)} %get-tuple-element.115), custom_call_target="InvertDiagBlocksLowerTriangular" | custom-call | tf_op jit(solution)/shard_map/jit(cholesky)/cholesky | solution.py:73
  100.8 1.6 convolution_subtract_fusion.1
  102.5 11.7 %cholesky.413 = f32[128,128]{1,0:T(8,128)S(1)} custom-call(f32[128,128]{1,0:T(8,128)S(1)} %cholesky.517), custom_call_target="Cholesky" | custom-call | tf_op jit(solution)/shard_map/jit(cholesky)/cholesky | solution.py:73
  114.8 9.8 %custom-call.58 = f32[1,128,128]{1,2,0:T(8,128)S(1)} custom-call(f32[1,128,128]{2,1,0:T(8,128)S(1)} %get-tuple-element.112), custom_call_target="InvertDiagBlocksLowerTriangular" | custom-call | tf_op jit(solution)/shard_map/jit(cholesky)/cholesky | solution.py:73
  125.0 1.7 convolution_subtract_fusion.2
  126.7 11.9 %cholesky.432 = f32[128,128]{1,0:T(8,128)S(1)} custom-call(f32[128,128]{1,0:T(8,128)S(1)} %cholesky.522), custom_call_target="Cholesky" | custom-call | tf_op jit(solution)/shard_map/jit(cholesky)/cholesky | solution.py:73
  139.4 9.8 %custom-call.59 = f32[1,128,128]{1,2,0:T(8,128)S(1)} custom-call(f32[1,128,128]{2,1,0:T(8,128)S(1)} %get-tuple-element.109), custom_call_target="InvertDiagBlocksLowerTriangular" | custom-call | tf_op jit(solution)/shard_map/jit(cholesky)/cholesky | solution.py:73
  149.5 1.7 convolution_subtract_fusion.3
  151.2 11.7 %cholesky.451 = f32[128,128]{1,0:T(8,128)S(1)} custom-call(f32[128,128]{1,0:T(8,128)S(1)} %cholesky.527), custom_call_target="Cholesky" | custom-call | tf_op jit(solution)/shard_map/jit(cholesky)/cholesky | solution.py:73
  163.6 9.8 %custom-call.60 = f32[1,128,128]{1,2,0:T(8,128)S(1)} custom-call(f32[1,128,128]{2,1,0:T(8,128)S(1)} %get-tuple-element.106), custom_call_target="InvertDiagBlocksLowerTriangular" | custom-call | tf_op jit(solution)/shard_map/jit(cholesky)/cholesky | solution.py:73
  173.7 1.5 convolution_subtract_fusion.4
  175.3 12.2 %cholesky.471 = f32[128,128]{1,0:T(8,128)S(1)} custom-call(f32[128,128]{1,0:T(8,128)S(1)} %cholesky.532), custom_call_target="Cholesky" | custom-call | tf_op jit(solution)/shard_map/jit(cholesky)/cholesky | solution.py:73
  188.1 9.8 %custom-call.61 = f32[1,128,128]{1,2,0:T(8,128)S(1)} custom-call(f32[1,128,128]{2,1,0:T(8,128)S(1)} %get-tuple-element.103), custom_call_target="InvertDiagBlocksLowerTriangular" | custom-call | tf_op jit(solution)/shard_map/jit(cholesky)/cholesky | solution.py:73
  199.3 8.6 %cholesky.492 = f32[94,94]{1,0:T(8,128)S(1)} custom-call(f32[94,94]{1,0:T(8,128)S(1)} %convolution_subtract_fusion.5), custom_call_target="Cholesky" | custom-call | tf_op jit(solution)/shard_map/jit(cholesky)/cholesky | solution.py:73
  215.6 17.4 %while.4 = (s32[]{:T(128)}, f32[862,862]{1,0:T(8,128)}, s32[6,2]{0,1:T(2,128)S(1)}, f32[6,128,128]{2,1,0:T(8,128)S(1)}, s32[]{:T(128)}) while((s32[]{:T(128)}, f32[862,862]{1,0:T(8,128)}, s32[6,2]{0,1:T(2,128)S(1)}, f32[6,128,128]{2,1,0:T(8,128)S(1)}, s32[]{:T(128)}) %tuple.121), condition=%wide.while_cond.clone, body=%wide.while_body.clone.sunk | while | flops 2 | bytes 131181 | solution.py:53
  216.2 2.3 bitcast_dynamic-update-slice_fusion.2
  219.1 2.3 bitcast_dynamic-update-slice_fusion.2
  222.0 2.3 bitcast_dynamic-update-slice_fusion.2
  224.9 2.3 bitcast_dynamic-update-slice_fusion.2
  227.8 2.3 bitcast_dynamic-update-slice_fusion.2
  230.7 2.3 bitcast_dynamic-update-slice_fusion.2
  234.0 69.9 %custom-call.64 = f32[7,128,128]{1,2,0:T(8,128)S(1)} custom-call(f32[7,128,128]{2,1,0:T(8,128)} %pad_maximum_fusion), custom_call_target="InvertDiagBlocksLowerTriangular" | custom-call | tf_op jit(solution)/shard_map/jit(_cho_solve)/triangular_solve | solution.py:53
  303.9 3.1 convolution_multiply_fusion
  317.9 131.3 %all-gather.7.cloned.1.call-done = f32[128,20,862]{2,1,0:T(8,128)} async-done(((f32[1,20,862]{2,1,0:T(8,128)}), f32[128,20,862]{2,1,0:T(8,128)}) %all-gather.7.cloned.1.call-update) | async-done | bytes 8826896 | tf_op jit(solution)/shard_map/all_gather | solution.py:14
  449.2 5.4 reduce_sum.198
  462.2 1.5 fusion.108
  467.7 124.5 %all-gather.9.cloned.1.call-done = f32[128,20,862]{2,1,0:T(8,128)} async-done(((f32[1,20,862]{2,1,0:T(8,128)}), f32[128,20,862]{2,1,0:T(8,128)}) %all-gather.9.cloned.1.call-update) | async-done | bytes 8826896 | tf_op jit(solution)/shard_map/all_gather | solution.py:14
  592.1 4.8 reduce_sum.199
  596.9 1.6 multiply_reduce_fusion.2
  604.7 11.7 %all-reduce.19 = (f32[8]{0:T(128)S(1)}, f32[8]{0:T(128)S(1)}, f32[8]{0:T(128)S(1)}, f32[8]{0:T(128)S(1)}) all-reduce(f32[8]{0:T(128)S(1)} %dynamic-update-slice.54, f32[8]{0:T(128)S(1)} %dynamic-update-slice.50, f32[8]{0:T(128)S(1)} %dynamic-update-slice.46, ...), channel_id=1, replica_groups=mesh['slab_0'=8,'slab_1'=4,'slab_2'=4,'feat'=2] {'slab_0'}, use_global_device_ids=true, to_apply=%add.15 | all-reduce | flops 32 | bytes 256
  624.8 8.4 %all-reduce.21 = (f32[4]{0:T(128)S(1)}, f32[4]{0:T(128)S(1)}, f32[4]{0:T(128)S(1)}, f32[4]{0:T(128)S(1)}) all-reduce(f32[4]{0:T(128)S(1)} %dynamic-update-slice.55, f32[4]{0:T(128)S(1)} %dynamic-update-slice.51, f32[4]{0:T(128)S(1)} %dynamic-update-slice.47, ...), channel_id=1, replica_groups=mesh['slab_0'=8,'slab_1'=4,'slab_2'=4,'feat'=2] {'slab_1'}, use_global_device_ids=true, to_apply=%add.16 | all-reduce | flops 16 | bytes 128
  642.0 6.6 all-reduce.20
  649.8 1.4 dynamic-update-slice.45
  651.3 1.4 dynamic-update-slice.49
  653.3 1.4 dynamic-update-slice.53
  655.4 1.4 dynamic-update-slice.57
  657.5 11.2 %all-reduce.22 = (f32[2]{0:T(128)S(1)}, f32[2]{0:T(128)S(1)}, f32[2]{0:T(128)S(1)}, f32[2]{0:T(128)S(1)}) all-reduce(f32[2]{0:T(128)S(1)} %dynamic-update-slice.57, f32[2]{0:T(128)S(1)} %dynamic-update-slice.53, f32[2]{0:T(128)S(1)} %dynamic-update-slice.49, ...), channel_id=1, replica_groups=mesh['slab_0'=8,'slab_1'=4,'slab_2'=4,'feat'=2] {'feat'}, use_global_device_ids=true, to_apply=%add.18 | all-reduce | flops 8 | bytes 64
  (257 shorter events, 80.4 us)
Async XLA Ops:
  7.2 442.0 %all-gather.7.cloned.1.call-start = ((), (), s32[]{:S(2)}) async-start(), calls=%async_computation | async-start | bytes 11096064 | tf_op jit(solution)/shard_map/all_gather | solution.py:14
  35.5 7.8 %copy-start = (f32[862,512]{1,0:T(8,128)}, f32[862,512]{1,0:T(8,128)S(1)}, u32[]{:S(2)}) copy-start(f32[862,512]{1,0:T(8,128)S(1)} %concatenate.49) | copy-start | bytes 5296132
  49.4 1.6 copy-start.3
  213.7 0.7 copy-start.11
  213.7 1.9 copy-start.7
  213.7 19.3 %copy-start.9 = (pred[34,34]{1,0:T(8,128)(4,1)S(1)}, pred[34,34]{1,0:T(8,128)(4,1)}, u32[]{:S(2)}) copy-start(pred[34,34]{1,0:T(8,128)(4,1)} %iota_compare_fusion.7) | copy-start | bytes 3472
  214.0 1.6 copy-start.1
  233.1 74.1 %copy-start.2 = (f32[862,862]{1,0:T(8,128)S(1)}, f32[862,862]{1,0:T(8,128)}, u32[]{:S(2)}) copy-start(f32[862,862]{1,0:T(8,128)} %get-tuple-element.215) | copy-start | bytes 8916532
  307.0 10.8 %copy-start.6 = (f32[862,20]{0,1:T(8,128)}, f32[862,20]{0,1:T(8,128)S(1)}, u32[]{:S(2)}) copy-start(f32[862,20]{0,1:T(8,128)S(1)} %convolution_multiply_fusion) | copy-start | bytes 206884
  317.8 274.3 %all-gather.9.cloned.1.call-start = ((), (), s32[]{:S(2)}) async-start(), calls=%async_computation.1 | async-start | bytes 11096064 | tf_op jit(solution)/shard_map/all_gather | solution.py:14
  454.6 7.6 %copy-start.4 = (f32[20,862]{1,0:T(8,128)S(1)}, f32[20,862]{1,0:T(8,128)}, u32[]{:S(2)}) copy-start(f32[20,862]{1,0:T(8,128)} %reduce_sum.198) | copy-start | bytes 206884
  467.6 129.2 %copy-start.5 = (f32[20,862]{1,0:T(8,128)S(1)}, f32[20,862]{1,0:T(8,128)}, u32[]{:S(2)}) copy-start(f32[20,862]{1,0:T(8,128)} %reduce_sum.198) | copy-start | bytes 206884
  467.7 136.4 %copy-start.10 = (u32[256]{0:T(256)S(1)}, u32[256]{0:T(256)}, u32[]{:S(2)}) copy-start(u32[256]{0:T(256)} %constant.325) | copy-start | bytes 3076
  598.5 76.1 %copy-start.8 = (f32[20,862]{1,0:T(8,128)}, f32[20,862]{1,0:T(8,128)S(1)}, u32[]{:S(2)}) copy-start(f32[20,862]{1,0:T(8,128)S(1)} %get-tuple-element.57) | copy-start | bytes 206884
Sparse Core Ops, SparseCore 0:
  317.9 131.2 all-gather.6
  463.9 128.1 all-gather.8
